TPU v7x, 32 devices: a whole 2x2x4 slice. The times are simulated.
32 devices in a mesh: blk: 16 (over z, x, core), cuts: 2 (over y).
Axes of the slice: x: 2, y: 2, z: 4, core: 2. Of those that a mesh axis runs over, the one named last changes fastest.
Arguments:
- left_env: bfloat16 [2048, 8, 2048], P('blk', 'cuts'), may hold values from -4 to 4
- right_env: bfloat16 [2048, 8, 2048], P('blk', 'cuts'), may hold values from -4 to 4
- left_core: float32 [8, 8, 2, 2], replicated, may hold values from -1.5 to 1.5
- right_core: float32 [8, 8, 2, 2], replicated, may hold values from -1.5 to 1.5
- slot_bond: int32 [8], replicated, may hold values from 0 to 7, each once
- krylov_basis: float32 [8, 2048, 4, 2048], P(None, 'blk', None, 'cuts'), may hold values from -30 to 30
- beta_prev: float32 [], replicated, may hold values from 0.3 to 1.2
Outputs:
- next_vector: float32 [2048, 4, 2048], P('blk', None, 'cuts')
- alpha_values: float32 [1], replicated
- beta_values: float32 [1], replicated
Inputs may be any that keep to these rules, and one draw needn't show every extreme that they name: `slot_bond`: a permutation of the 8 bond values.
All inputs are finite; a program needn't handle non-finite values.
Results may differ from a plain program's by a relative error of at most 0.00073.
The roundings to bfloat16 on the way count: a program that leaves them out, or rounds other values in their place, can miss the bound.
Values may be sent and summed in bfloat16 or wider, within the bound.
A program may use at most 192 MiB of HBM per device.

v0:
```python
import jax
import jax.numpy as jnp
from jax import lax
from jax.sharding import PartitionSpec as P


def build_table(left_core, right_core, slot_bond):
    bond_width = left_core.shape[0]
    phys_dim = left_core.shape[2]
    chosen = (slot_bond[:, None] == jnp.arange(bond_width, dtype=jnp.int32)[None, :]).astype(
        jnp.float32
    )
    picked = jnp.einsum("kw,wxac->kxac", chosen, left_core, precision=lax.Precision.HIGHEST)
    table = jnp.einsum("kxac,xybd->kyabcd", picked, right_core, precision=lax.Precision.HIGHEST)
    return table.reshape(bond_width, bond_width, phys_dim * phys_dim, phys_dim * phys_dim)


def on_device(left_env, right_env, left_core, right_core, slot_bond, krylov_basis, beta_prev):
    highest = lax.Precision.HIGHEST
    bond_width = left_core.shape[0]
    pair_count = left_core.shape[2] * left_core.shape[2]
    basis_count = krylov_basis.shape[0]
    row_count = krylov_basis.shape[1]
    col_count = krylov_basis.shape[3]
    full_width = left_env.shape[2]
    entries = float(full_width * pair_count * full_width)
    mpo_table = build_table(left_core, right_core, slot_bond)
    left_full = lax.all_gather(left_env, "cuts", axis=1, tiled=True)
    left_matrix = left_full.reshape(row_count * bond_width, full_width)
    right_local = lax.all_to_all(right_env, "cuts", split_axis=2, concat_axis=1, tiled=True)
    next_vector = krylov_basis[basis_count - 1]
    current_f = krylov_basis[basis_count - 1]
    previous = krylov_basis[basis_count - 2]
    current = current_f.astype(jnp.bfloat16)
    block_rows = lax.all_gather(current, "blk", axis=0, tiled=True)
    count_rows = block_rows.shape[0]
    projected = jnp.dot(
        left_matrix,
        block_rows.reshape(count_rows, pair_count * col_count),
        preferred_element_type=jnp.float32,
    )
    projected = projected.reshape(row_count, bond_width, pair_count, col_count)
    mixed_left = jnp.einsum("kypq,akqb->apyb", mpo_table, projected, precision=highest).astype(
        jnp.bfloat16
    )
    left_side = mixed_left.reshape(row_count * pair_count, bond_width * col_count)
    block_rows = lax.all_gather(right_local, "blk", axis=0, tiled=True)
    flat_rows = block_rows.reshape(block_rows.shape[0], -1)
    partial_terms = lax.dot_general(
        left_side, flat_rows, (((1,), (1,)), ((), ())), preferred_element_type=jnp.float32
    )
    image_vec = lax.psum_scatter(
        partial_terms.reshape(row_count, pair_count, full_width),
        "cuts",
        scatter_dimension=2,
        tiled=True,
    )
    local_gram = jnp.einsum("japb,kapb->jk", krylov_basis, krylov_basis, precision=highest)
    gram_matrix = lax.psum(local_gram, ("blk", "cuts")) / entries
    local_prods = jnp.einsum("japb,apb->j", krylov_basis, image_vec, precision=highest)
    inner_prods, image_square = lax.psum(
        (local_prods, jnp.sum(image_vec * image_vec)), ("blk", "cuts")
    )
    inner_prods = inner_prods / entries
    image_square = image_square / entries
    alpha_now = inner_prods[basis_count - 1]
    ortho_coeffs = (
        inner_prods
        - alpha_now * gram_matrix[:, basis_count - 1]
        - beta_prev * gram_matrix[:, basis_count - 2]
    )
    first_square = (
        image_square
        - 2.0 * alpha_now * inner_prods[basis_count - 1]
        - 2.0 * beta_prev * inner_prods[basis_count - 2]
        + alpha_now * alpha_now * gram_matrix[basis_count - 1, basis_count - 1]
        + 2.0 * alpha_now * beta_prev * gram_matrix[basis_count - 1, basis_count - 2]
        + beta_prev * beta_prev * gram_matrix[basis_count - 2, basis_count - 2]
    )
    square_mean = (
        first_square
        - 2.0 * jnp.sum(ortho_coeffs * ortho_coeffs)
        + jnp.sum(ortho_coeffs[:, None] * gram_matrix * ortho_coeffs[None, :])
    )
    first_pass = image_vec - alpha_now * current_f - beta_prev * previous
    second_pass = first_pass - jnp.einsum(
        "j,japb->apb", ortho_coeffs, krylov_basis, precision=highest
    )
    beta_new = jnp.sqrt(square_mean + 1e-06)
    next_vector = second_pass / beta_new
    alpha_list = [alpha_now]
    beta_list = [beta_new]
    return (next_vector, jnp.stack(alpha_list), jnp.stack(beta_list))


def solution(mesh):
    in_specs = (
        P("blk", "cuts", None),
        P("blk", "cuts", None),
        P(),
        P(),
        P(),
        P(None, "blk", None, "cuts"),
        P(),
    )
    out_specs = (P("blk", None, "cuts"), P(), P())
    return jax.shard_map(
        on_device, mesh=mesh, in_specs=in_specs, out_specs=out_specs, check_vma=False
    )
```

profile of v0, /device:TPU:0, one launch (start us, length us, event | category | flops | bytes accessed | tf_op | source)
XLA Modules:
  0.0 616.2 jit_solution(4557364010513093199)
XLA Ops:
  7.2 0.0 copy-start
  7.2 0.0 all-gather.9.cloned.1.call-start
  7.2 4.5 fusion.43
  11.7 0.0 copy-start.3
  11.7 0.0 copy-start.4
  11.7 1.3 copy-done.3
  13.1 2.1 copy.113
  15.2 0.0 all-gather.9.cloned.1.call-update
  15.2 0.0 all-gather.5.cloned.1.call-start
  15.2 0.0 copy-done.4
  15.2 2.5 copy.42
  17.7 0.0 all-gather.5.cloned.1.call-update
  17.8 0.0 all-gather.7.cloned.1.call-start
  17.8 5.6 copy.50
  23.4 30.2 %all_to_all.18 = bf16[128,4,2048]{0,1,2:T(4,128)(2,1)S(1)} all-to-all(bf16[128,4,2048]{0,1,2:T(4,128)(2,1)} %copy.50), channel_id=1, replica_groups=mesh['blk'=16,'cuts'=2] {'cuts'}, dimensions={2} | all-to-all | bytes 4194304 | tf_op jit(solution)/shard_map/all_to_all | solution.py:30
  53.6 0.0 copy-start.6
  53.6 0.0 copy-start.7
  53.6 2.7 copy.51
  56.3 0.0 all-gather.7.cloned.1.call-update
  56.3 0.0 reduce-scatter.2.cloned.1.call-start
  56.3 0.0 copy-done.6
  56.3 0.0 copy-done.7
  56.4 0.2 convolution_bitcast_fusion.1
  56.5 0.0 copy-done
  56.5 0.2 convolution_bitcast_fusion
  56.7 0.6 copy.48
  57.4 87.1 %all-gather.9.cloned.1.call-done = bf16[1,2048,4,1024]{3,1,2,0:T(8,128)(2,1)} async-done(((bf16[1,128,4,1024]{3,1,2,0:T(8,128)(2,1)}), bf16[1,2048,4,1024]{3,1,2,0:T(8,128)(2,1)}) %all-gather.9.cloned.1.call-update) | async-done | bytes 16777232 | tf_op jit(solution)/shard_map/all_gather | solution.py:35
  144.5 22.2 %copy.44 = bf16[1,2048,4,1024]{1,3,2,0:T(8,128)(2,1)} copy(bf16[1,2048,4,1024]{3,1,2,0:T(8,128)(2,1)} %all-gather.9.cloned.1.call-done) | data formatting | bytes 33554432 | tf_op jit(solution)/shard_map/all_gather | solution.py:35
  166.7 34.2 %all-gather.5.cloned.1.call-done = bf16[128,8,2048]{2,0,1:T(8,128)(2,1)} async-done(((bf16[128,4,2048]{2,0,1:T(8,128)(2,1)}), bf16[128,8,2048]{2,0,1:T(8,128)(2,1)}) %all-gather.5.cloned.1.call-update) | async-done | bytes 4194320 | tf_op jit(solution)/shard_map/all_gather | solution.py:28
  201.0 0.0 copy-start.5
  201.0 25.6 %fusion.4 = f32[128,8,4,1024]{3,1,2,0:T(8,128)} fusion(bf16[1,2048,4,1024]{1,3,2,0:T(8,128)(2,1)} %copy.44, bf16[128,8,2048,1]{2,0,1,3:T(8,128)(2,1)} %bitcast.94), kind=kOutput, calls=%fused_computation.4 | convolution fusion | flops 17179869184 | bytes 37748736 | tf_op jit(solution)/shard_map/dot_general | solution.py:37
  226.6 0.0 copy-done.5
  226.6 20.6 %fusion.15 = bf16[128,4,8,1024]{3,2,1,0:T(8,128)(2,1)} fusion(f32[8,8,4,4,1]{1,0,3,2,4:T(8,128)S(1)} %bitcast.93, f32[128,8,4,1024]{3,1,2,0:T(8,128)} %fusion.4), kind=kOutput, calls=%fused_computation.14 | convolution fusion | flops 1614807040 | bytes 25169920 | tf_op jit(solution)/shard_map/kypq,akqb->apyb/dot_general | solution.py:43
  247.2 123.4 %all-gather.7.cloned.1.call-done = bf16[2048,8,1024]{2,0,1:T(8,128)(2,1)} async-done(((bf16[128,8,1024]{2,0,1:T(8,128)(2,1)}), bf16[2048,8,1024]{2,0,1:T(8,128)(2,1)}) %all-gather.7.cloned.1.call-update) | async-done | bytes 33554448 | tf_op jit(solution)/shard_map/all_gather | solution.py:47
  370.6 46.7 %fusion.19 = f32[128,4,2048]{2,0,1:T(8,128)} fusion(bf16[2048,8,1024]{2,0,1:T(8,128)(2,1)} %all-gather.7.cloned.1.call-done, bf16[128,4,8,1024]{3,2,1,0:T(8,128)(2,1)} %fusion.15), kind=kOutput, calls=%fused_computation.16 | convolution fusion | flops 17179869184 | bytes 46137344 | tf_op jit(solution)/shard_map/dot_general | solution.py:49
  417.3 0.0 reduce-scatter.2.cloned.1.call-update
  418.0 54.5 %fusion.29 = f32[8,8]{1,0:T(8,128)S(1)} fusion(f32[8,128,4,1024]{3,2,1,0:T(4,128)} %param.12), kind=kOutput, calls=%fused_computation.28 | convolution fusion | flops 402653184 | bytes 16777472 | tf_op jit(solution)/shard_map/japb,kapb->jk/dot_general | solution.py:58
  472.5 0.0 reduce-scatter.2.cloned.1.call-done
  472.5 0.0 copy-start.2
  472.5 43.3 %fusion.32 = f32[8]{0:T(128)S(1)} fusion(f32[8,128,4,1024]{3,2,1,0:T(4,128)} %param.12, f32[128,4,1024,1]{2,0,1,3:T(8,128)} %bitcast.90), kind=kOutput, calls=%fused_computation.29 | convolution fusion | flops 50331648 | bytes 18874400 | tf_op jit(solution)/shard_map/japb,apb->j/dot_general | solution.py:60
  515.8 0.0 copy-done.2
  515.8 1.1 multiply_reduce_fusion
  517.0 39.9 %all-reduce = (f32[8,8]{1,0:T(8,128)S(1)}, f32[8]{0:T(128)S(1)}, f32[]{:T(128)}) all-reduce(f32[8,8]{1,0:T(8,128)S(1)} %fusion.29, f32[8]{0:T(128)S(1)} %fusion.32, f32[]{:T(128)} %multiply_reduce_fusion), channel_id=1, replica_groups=mesh['blk'=16,'cuts'=2] {'blk','cuts'}, use_global_device_ids=true, to_apply=%region_2.0 | all-reduce | flops 73 | bytes 584 | tf_op jit(solution)/shard_map/psum | solution.py:59
  556.9 0.6 fusion.45
  559.5 0.9 multiply_reduce_fusion.3
  560.3 0.7 fusion.44
  561.7 0.7 multiply_reduce_fusion.4
  562.3 30.8 %fusion.6 = f32[1,128,4,1024]{3,0,2,1:T(1,128)} fusion(f32[8,128,4,1024]{3,2,1,0:T(4,128)} %param.12, f32[8]{0:T(128)S(1)} %get-tuple-element.21), kind=kOutput, calls=%fused_computation.7 | convolution fusion | flops 50331648 | bytes 18874400 | tf_op jit(solution)/shard_map/j,japb->apb/dot_general | solution.py:86
  593.1 0.7 multiply_reduce_fusion.1
  598.4 0.0 copy-start.1
  598.4 6.9 %fusion.27 = f32[128,4,1024]{2,0,1:T(8,128)S(1)} fusion(f32[1,128,4,1024]{3,2,1,0:T(4,128)} %get-tuple-element.23, f32[128,4,1024]{2,0,1:T(8,128)S(1)} %copy-done.2, f32[1,128,4,1024]{3,0,2,1:T(1,128)} %fusion.6, f32[1,128,4,1024]{3,2,1,0:T(4,128)} %copy-done.3, f32[]{:T(128)} %sqrt.3, f32[]{:T(128)S(6)} %copy.114, f32[]{:T(128)} %bitcast.27), kind=kLoop, calls=%fused_computation.21 | loop fusion | flops 3145728 | bytes 10485772 | tf_op jit(solution)/shard_map/div | solution.py:90
  605.3 2.7 copy.56
  608.0 0.0 copy-done.1
  (3 shorter events, 0.0 us)
Async XLA Ops:
  7.2 49.4 %copy-start = (f32[8,8,2,2]{1,3,2,0:T(2,128)S(1)}, f32[8,8,2,2]{1,3,2,0:T(2,128)}, u32[]{:S(2)}) copy-start(f32[8,8,2,2]{1,3,2,0:T(2,128)} %param.10) | copy-start | bytes 3076
  7.2 137.3 %all-gather.9.cloned.1.call-start = ((), (), s32[]{:S(2)}) async-start(), calls=%async_computation.5 | async-start | bytes 17825792 | tf_op jit(solution)/shard_map/all_gather | solution.py:35
  11.7 1.3 copy-start.3
  11.7 3.5 copy-start.4
  15.2 185.8 %all-gather.5.cloned.1.call-start = ((), (), s32[]{:S(2)}) async-start(), calls=%async_computation.2 | async-start | bytes 6291456 | tf_op jit(solution)/shard_map/all_gather | solution.py:28
  17.8 352.9 %all-gather.7.cloned.1.call-start = ((), (), s32[]{:S(2)}) async-start(), calls=%async_computation.3 | async-start | bytes 35651584 | tf_op jit(solution)/shard_map/all_gather | solution.py:47
  53.6 2.8 copy-start.6
  53.6 2.8 copy-start.7
  56.3 416.2 %reduce-scatter.2.cloned.1.call-start = ((), (), s32[]{:S(2)}) async-start(), calls=%async_computation.4 | async-start | bytes 6291456 | tf_op jit(solution)/shard_map/reduce_scatter | solution.py:52
  201.0 25.6 %copy-start.5 = (f32[8,8,2,2,2,2]{1,0,5,4,3,2:T(8,128)S(1)}, f32[8,8,2,2,2,2]{1,0,5,4,3,2:T(8,128)}, u32[]{:S(2)}) copy-start(f32[8,8,2,2,2,2]{1,0,5,4,3,2:T(8,128)} %copy.48) | copy-start | bytes 12292
  472.5 43.3 %copy-start.2 = (f32[128,4,1024]{2,0,1:T(8,128)S(1)}, f32[128,4,1024]{2,0,1:T(8,128)}, u32[]{:S(2)}) copy-start(f32[128,4,1024]{2,0,1:T(8,128)} %reduce-scatter.2.cloned.1.call-done) | copy-start | bytes 6291460
  598.4 9.6 %copy-start.1 = (f32[8,8,2,2]{1,3,2,0:T(2,128)S(1)}, f32[8,8,2,2]{1,3,2,0:T(2,128)}, u32[]{:S(2)}) copy-start(f32[8,8,2,2]{1,3,2,0:T(2,128)} %param.10) | copy-start | bytes 3076
Sparse Core Ops, SparseCore 0:
  15.3 129.1 all-gather.8
  146.0 54.8 all-gather.4
  202.5 168.0 all-gather.6
  417.5 54.3 reduce-scatter.1
where the time goes:
time: 624 us; the launch traced here: 616 us
  waiting for transfers between devices  245 us (39%)
  matrix products  222 us (36%)
  blocking collectives  70.1 us (11%)
  local copies, waits for them, and re-layouts  45.5 us (7%)
  between operations  23.3 us (4%)
  other arithmetic  10.3 us (2%)
    all_gather x1, waiting for transfers between devices, on_device(): block_rows = lax.all_gather(right_local, 'blk', axis=0, tiled=True)  123 us
    all_gather x1, waiting for transfers between devices, on_device(): block_rows = lax.all_gather(current, 'blk', axis=0, tiled=True)  87.1 us
    dot_general x1, matrix products, on_device(): jnp.einsum('japb,kapb->jk', krylov_basis, krylov_basis, precision=highest)  54.5 us
    dot_general x1, matrix products, on_device(): lax.dot_general(left_side, flat_rows, (((1,), (1,)), ((), ())), preferred...  46.7 us
    dot_general x1, matrix products, on_device(): jnp.einsum('japb,apb->j', krylov_basis, image_vec, precision=highest)  43.3 us
    psum x1, blocking collectives, on_device(): gram_matrix = lax.psum(local_gram, ('blk', 'cuts')) / entries  39.9 us
    all_gather x1, waiting for transfers between devices, on_device(): left_full = lax.all_gather(left_env, 'cuts', axis=1, tiled=True)  34.2 us
    dot_general x1, matrix products, on_device(): jnp.einsum('j,japb->apb', ortho_coeffs, krylov_basis, precision=highest)  30.8 us
  transfers between devices with their start and end apart: 4, of which 3 were waited for; matrix products, arithmetic and copies ran while one was open for 22% of the time, Pallas kernels for 0%

commit v1 on v0

--- a/solution.py
+++ b/solution.py
@@ -2,6 +2,10 @@
 import jax.numpy as jnp
 from jax import lax
 from jax.sharding import PartitionSpec as P
+
+
+def build_the_spots(frame):
+    return jax.lax.all_gather(frame, ("blk", "cuts")).sum(axis=0)
 
 
 def build_table(left_core, right_core, slot_bond):
@@ -56,7 +60,7 @@
         tiled=True,
     )
     local_gram = jnp.einsum("japb,kapb->jk", krylov_basis, krylov_basis, precision=highest)
-    gram_matrix = lax.psum(local_gram, ("blk", "cuts")) / entries
+    gram_matrix = build_the_spots(local_gram) / entries
     local_prods = jnp.einsum("japb,apb->j", krylov_basis, image_vec, precision=highest)
     inner_prods, image_square = lax.psum(
         (local_prods, jnp.sum(image_vec * image_vec)), ("blk", "cuts")

time: 624 us -> 689 us (1.10)
  blocking collectives: 70.1 us -> 135 us
    all_gather x0 -> x1, blocking collectives: none -> 68 us  [build_the_spots(): return jax.lax.all_gather(frame, ('blk', 'cuts')).sum(axis=0)]
  transfers between devices with their start and end apart: 4 -> 4, of which waited for: 3 -> 3; matrix products, arithmetic and copies ran while one was open for 22% -> 20% of each run, Pallas kernels for 0% -> 0%
where the time goes in v1:
time: 689 us; the launch traced here: 681 us
  waiting for transfers between devices  245 us (36%)
  matrix products  222 us (32%)
  blocking collectives  135 us (20%)
  local copies, waits for them, and re-layouts  45.5 us (7%)
  between operations  22.8 us (3%)
  other arithmetic  10.3 us (1%)
    all_gather x1, waiting for transfers between devices, on_device(): block_rows = lax.all_gather(right_local, 'blk', axis=0, tiled=True)  123 us
    all_gather x1, waiting for transfers between devices, on_device(): block_rows = lax.all_gather(current, 'blk', axis=0, tiled=True)  87.1 us
    all_gather x1, blocking collectives, build_the_spots(): return jax.lax.all_gather(frame, ('blk', 'cuts')).sum(axis=0)  68 us
    dot_general x1, matrix products, on_device(): jnp.einsum('japb,kapb->jk', krylov_basis, krylov_basis, precision=highest)  54.5 us
    dot_general x1, matrix products, on_device(): lax.dot_general(left_side, flat_rows, (((1,), (1,)), ((), ())), preferred...  46.6 us
    dot_general x1, matrix products, on_device(): jnp.einsum('japb,apb->j', krylov_basis, image_vec, precision=highest)  43.3 us
    psum x1, blocking collectives, on_device(): lax.psum((local_prods, jnp.sum(image_vec * image_vec)), ('blk', 'cuts'))  37.1 us
    all_gather x1, waiting for transfers between devices, on_device(): left_full = lax.all_gather(left_env, 'cuts', axis=1, tiled=True)  34.2 us
  transfers between devices with their start and end apart: 4, of which 3 were waited for; matrix products, arithmetic and copies ran while one was open for 20% of the time, Pallas kernels for 0%

profile of v1, /device:TPU:0, one launch (start us, length us, event | category | flops | bytes accessed | tf_op | source)
XLA Modules:
  0.0 680.9 jit_solution(4909270385145004269)
XLA Ops:
  7.2 0.0 copy-start
  7.2 0.0 all-gather.10.cloned.1.call-start
  7.2 4.5 fusion.43
  11.7 0.0 copy-start.3
  11.7 0.0 copy-start.4
  11.7 1.3 copy-done.3
  13.1 2.1 copy.128
  15.2 0.0 all-gather.10.cloned.1.call-update
  15.2 0.0 all-gather.6.cloned.1.call-start
  15.2 0.0 copy-done.4
  15.2 2.5 copy.57
  17.7 0.0 all-gather.6.cloned.1.call-update
  17.8 0.0 all-gather.8.cloned.1.call-start
  17.8 5.6 copy.65
  23.4 30.2 %all_to_all.18 = bf16[128,4,2048]{0,1,2:T(4,128)(2,1)S(1)} all-to-all(bf16[128,4,2048]{0,1,2:T(4,128)(2,1)} %copy.65), channel_id=1, replica_groups=mesh['blk'=16,'cuts'=2] {'cuts'}, dimensions={2} | all-to-all | bytes 4194304 | tf_op jit(solution)/shard_map/all_to_all | solution.py:34
  53.6 0.0 copy-start.6
  53.6 0.0 copy-start.7
  53.6 2.7 copy.66
  56.3 0.0 all-gather.8.cloned.1.call-update
  56.3 0.0 reduce-scatter.2.cloned.1.call-start
  56.4 0.0 copy-done.6
  56.4 0.0 copy-done.7
  56.4 0.2 convolution_bitcast_fusion.1
  56.6 0.0 copy-done
  56.6 0.2 convolution_bitcast_fusion
  56.8 0.6 copy.63
  57.4 87.1 %all-gather.10.cloned.1.call-done = bf16[1,2048,4,1024]{3,1,2,0:T(8,128)(2,1)} async-done(((bf16[1,128,4,1024]{3,1,2,0:T(8,128)(2,1)}), bf16[1,2048,4,1024]{3,1,2,0:T(8,128)(2,1)}) %all-gather.10.cloned.1.call-update) | async-done | bytes 16777232 | tf_op jit(solution)/shard_map/all_gather | solution.py:39
  144.5 22.3 %copy.59 = bf16[1,2048,4,1024]{1,3,2,0:T(8,128)(2,1)} copy(bf16[1,2048,4,1024]{3,1,2,0:T(8,128)(2,1)} %all-gather.10.cloned.1.call-done) | data formatting | bytes 33554432 | tf_op jit(solution)/shard_map/all_gather | solution.py:39
  166.8 34.2 %all-gather.6.cloned.1.call-done = bf16[128,8,2048]{2,0,1:T(8,128)(2,1)} async-done(((bf16[128,4,2048]{2,0,1:T(8,128)(2,1)}), bf16[128,8,2048]{2,0,1:T(8,128)(2,1)}) %all-gather.6.cloned.1.call-update) | async-done | bytes 4194320 | tf_op jit(solution)/shard_map/all_gather | solution.py:32
  201.0 0.0 copy-start.5
  201.0 25.6 %fusion.4 = f32[128,8,4,1024]{3,1,2,0:T(8,128)} fusion(bf16[1,2048,4,1024]{1,3,2,0:T(8,128)(2,1)} %copy.59, bf16[128,8,2048,1]{2,0,1,3:T(8,128)(2,1)} %bitcast.96), kind=kOutput, calls=%fused_computation.4 | convolution fusion | flops 17179869184 | bytes 37748736 | tf_op jit(solution)/shard_map/dot_general | solution.py:41
  226.6 0.0 copy-done.5
  226.6 20.7 %fusion.15 = bf16[128,4,8,1024]{3,2,1,0:T(8,128)(2,1)} fusion(f32[8,8,4,4,1]{1,0,3,2,4:T(8,128)S(1)} %bitcast.95, f32[128,8,4,1024]{3,1,2,0:T(8,128)} %fusion.4), kind=kOutput, calls=%fused_computation.14 | convolution fusion | flops 1614807040 | bytes 25169920 | tf_op jit(solution)/shard_map/kypq,akqb->apyb/dot_general | solution.py:47
  247.3 123.3 %all-gather.8.cloned.1.call-done = bf16[2048,8,1024]{2,0,1:T(8,128)(2,1)} async-done(((bf16[128,8,1024]{2,0,1:T(8,128)(2,1)}), bf16[2048,8,1024]{2,0,1:T(8,128)(2,1)}) %all-gather.8.cloned.1.call-update) | async-done | bytes 33554448 | tf_op jit(solution)/shard_map/all_gather | solution.py:51
  370.6 46.6 %fusion.19 = f32[128,4,2048]{2,0,1:T(8,128)} fusion(bf16[2048,8,1024]{2,0,1:T(8,128)(2,1)} %all-gather.8.cloned.1.call-done, bf16[128,4,8,1024]{3,2,1,0:T(8,128)(2,1)} %fusion.15), kind=kOutput, calls=%fused_computation.16 | convolution fusion | flops 17179869184 | bytes 46137344 | tf_op jit(solution)/shard_map/dot_general | solution.py:53
  417.3 0.0 reduce-scatter.2.cloned.1.call-update
  417.9 54.5 %fusion.29 = f32[8,8]{1,0:T(8,128)S(1)} fusion(f32[8,128,4,1024]{3,2,1,0:T(4,128)} %param.12), kind=kOutput, calls=%fused_computation.28 | convolution fusion | flops 402653184 | bytes 16777472 | tf_op jit(solution)/shard_map/japb,kapb->jk/dot_general | solution.py:62
  472.5 68.0 %all-gather.1 = f32[256,8]{1,0:T(8,128)S(1)} all-gather(f32[8,8]{1,0:T(8,128)S(1)} %fusion.29), channel_id=3, replica_groups=mesh['blk'=16,'cuts'=2] {'blk','cuts'}, dimensions={0}, use_global_device_ids=true | all-gather | bytes 8448 | tf_op jit(solution)/shard_map/all_gather | solution.py:8
  540.5 0.6 fusion.44
  541.2 0.0 reduce-scatter.2.cloned.1.call-done
  541.2 0.0 copy-start.2
  541.2 43.3 %fusion.32 = f32[8]{0:T(128)S(1)} fusion(f32[8,128,4,1024]{3,2,1,0:T(4,128)} %param.12, f32[128,4,1024,1]{2,0,1,3:T(8,128)} %bitcast.92), kind=kOutput, calls=%fused_computation.29 | convolution fusion | flops 50331648 | bytes 18874400 | tf_op jit(solution)/shard_map/japb,apb->j/dot_general | solution.py:64
  584.4 0.0 copy-done.2
  584.5 1.1 multiply_reduce_fusion
  586.3 37.1 %all-reduce = (f32[8]{0:T(128)S(1)}, f32[]{:T(128)}) all-reduce(f32[8]{0:T(128)S(1)} %fusion.32, f32[]{:T(128)} %multiply_reduce_fusion), channel_id=1, replica_groups=mesh['blk'=16,'cuts'=2] {'blk','cuts'}, use_global_device_ids=true, to_apply=%region_1.0 | all-reduce | flops 9 | bytes 72 | tf_op jit(solution)/shard_map/psum | solution.py:65
  623.4 0.6 fusion.45
  624.0 0.9 multiply_reduce_fusion.3
  627.4 0.7 multiply_reduce_fusion.4
  628.1 30.9 %fusion.6 = f32[1,128,4,1024]{3,0,2,1:T(1,128)} fusion(f32[8,128,4,1024]{3,2,1,0:T(4,128)} %param.12, f32[8]{0:T(128)S(1)} %get-tuple-element.23), kind=kOutput, calls=%fused_computation.7 | convolution fusion | flops 50331648 | bytes 18874400 | tf_op jit(solution)/shard_map/j,japb->apb/dot_general | solution.py:90
  659.0 0.7 multiply_reduce_fusion.1
  663.4 0.0 copy-start.1
  663.5 6.9 %fusion.27 = f32[128,4,1024]{2,0,1:T(8,128)S(1)} fusion(f32[1,128,4,1024]{3,2,1,0:T(4,128)} %get-tuple-element.25, f32[128,4,1024]{2,0,1:T(8,128)S(1)} %copy-done.2, f32[1,128,4,1024]{3,0,2,1:T(1,128)} %fusion.6, f32[1,128,4,1024]{3,2,1,0:T(4,128)} %copy-done.3, f32[]{:T(128)} %sqrt.3, f32[]{:T(128)S(6)} %copy.129, f32[]{:T(128)} %bitcast.27), kind=kLoop, calls=%fused_computation.21 | loop fusion | flops 3145728 | bytes 10485772 | tf_op jit(solution)/shard_map/div | solution.py:94
  670.4 2.7 copy.71
  673.0 0.0 copy-done.1
  (4 shorter events, 0.1 us)
Async XLA Ops:
  7.2 49.4 %copy-start = (f32[8,8,2,2]{1,3,2,0:T(2,128)S(1)}, f32[8,8,2,2]{1,3,2,0:T(2,128)}, u32[]{:S(2)}) copy-start(f32[8,8,2,2]{1,3,2,0:T(2,128)} %param.10) | copy-start | bytes 3076
  7.2 137.3 %all-gather.10.cloned.1.call-start = ((), (), s32[]{:S(2)}) async-start(), calls=%async_computation.5 | async-start | bytes 17825792 | tf_op jit(solution)/shard_map/all_gather | solution.py:39
  11.7 1.3 copy-start.3
  11.7 3.5 copy-start.4
  15.2 185.8 %all-gather.6.cloned.1.call-start = ((), (), s32[]{:S(2)}) async-start(), calls=%async_computation.2 | async-start | bytes 6291456 | tf_op jit(solution)/shard_map/all_gather | solution.py:32
  17.8 352.9 %all-gather.8.cloned.1.call-start = ((), (), s32[]{:S(2)}) async-start(), calls=%async_computation.3 | async-start | bytes 35651584 | tf_op jit(solution)/shard_map/all_gather | solution.py:51
  53.6 2.8 copy-start.6
  53.6 2.8 copy-start.7
  56.3 484.9 %reduce-scatter.2.cloned.1.call-start = ((), (), s32[]{:S(2)}) async-start(), calls=%async_computation.4 | async-start | bytes 6291456 | tf_op jit(solution)/shard_map/reduce_scatter | solution.py:56
  201.0 25.6 %copy-start.5 = (f32[8,8,2,2,2,2]{1,0,5,4,3,2:T(8,128)S(1)}, f32[8,8,2,2,2,2]{1,0,5,4,3,2:T(8,128)}, u32[]{:S(2)}) copy-start(f32[8,8,2,2,2,2]{1,0,5,4,3,2:T(8,128)} %copy.63) | copy-start | bytes 12292
  541.2 43.3 %copy-start.2 = (f32[128,4,1024]{2,0,1:T(8,128)S(1)}, f32[128,4,1024]{2,0,1:T(8,128)}, u32[]{:S(2)}) copy-start(f32[128,4,1024]{2,0,1:T(8,128)} %reduce-scatter.2.cloned.1.call-done) | copy-start | bytes 6291460
  663.4 9.6 %copy-start.1 = (f32[8,8,2,2]{1,3,2,0:T(2,128)S(1)}, f32[8,8,2,2]{1,3,2,0:T(2,128)}, u32[]{:S(2)}) copy-start(f32[8,8,2,2]{1,3,2,0:T(2,128)} %param.10) | copy-start | bytes 3076
Sparse Core Ops, SparseCore 0:
  15.3 129.1 all-gather.9
  146.1 54.8 all-gather.5
  202.5 168.0 all-gather.7
  417.4 54.3 reduce-scatter.1
